TPU v7x, 32 devices: a whole 2x2x4 slice. The times are simulated.
32 devices in a mesh: grp: 2 (over x), tok: 8 (over z, y), side: 2 (over core).
Axes of the slice: x: 2, y: 2, z: 4, core: 2. Of those that a mesh axis runs over, the one named last changes fastest.
Arguments:
- hidden_in: bfloat16 [512, 3072], P(('grp', 'tok')), parts along dimension 0, may hold values from -6 to 6
- queries: bfloat16 [512, 24, 128], P(('grp', 'tok'), 'side'), parts along dimension 0, may hold values from -32 to 32
- key_new: bfloat16 [512, 4, 128], P(('grp', 'tok'), 'side'), parts along dimension 0, may hold values from -32 to 32
- value_new: bfloat16 [512, 4, 128], P(('grp', 'tok'), 'side'), parts along dimension 0, may hold values from -6 to 6
- cache_keys: bfloat16 [512, 4, 128, 128], P(('grp', 'tok'), 'side'), parts along dimension 0, may hold values from -32 to 32
- cache_values: bfloat16 [512, 4, 128, 128], P(('grp', 'tok'), 'side'), parts along dimension 0, may hold values from -6 to 6
- lengths: int32 [512], P(('grp', 'tok')), parts along dimension 0, may hold values from 1 to 128, 16384 in all
- out_weight: bfloat16 [3072, 3072], P('side', 'tok'), may hold values from -0.109375 to 0.109375
- norm_gain: float32 [3072], replicated, may hold values from 0.1 to 1.9
- router_weight: float32 [3072, 4], replicated, may hold values from -0.109375 to 0.109375
- gate_weight: bfloat16 [3072, 32768], P(None, ('tok', 'side')), may hold values from -0.109375 to 0.109375
- up_weight: bfloat16 [3072, 32768], P(None, ('tok', 'side')), may hold values from -0.109375 to 0.109375
- down_weight: bfloat16 [32768, 3072], P(('tok', 'side')), may hold values from -0.0625 to 0.0625
- routes: int32 [512, 2], P('grp'), parts along dimension 0, may hold values from 0 to 3, all different within a row; in each aligned block of 32 rows (0 to 31, 32 to 63, ...) at most 24 rows name the same one
Outputs:
- mixed: bfloat16 [512, 3072], P(('grp', 'tok')), parts along dimension 0
There are 2 independent parts, one for each index of `grp`. A program takes and returns all parts, laid end to end along the dimension named above; an argument that names none is the same for every part. Nothing has to cross between parts.
Inputs may be any that keep to these rules, and one draw needn't show every extreme that they name: Every sequence has at least one valid cache position and some sequence has 128; in each serving group the lengths sum to 16384. `routes`: each row names two different experts; among the rows of one index of tok (aligned blocks of 32 rows) no expert is named by more than 24 rows, and some expert reaches 24 in some block.
All inputs are finite; a program needn't handle non-finite values.
Results may differ from a plain program's by a relative error of at most 0.0075.
Values may be sent and summed in bfloat16 or wider, within the bound.
No kernel may reach another device: no remote copies, remote signals or barrier semaphores. Data moves between devices by JAX's collectives and lax.ppermute only.
A program may use at most 128 MiB of HBM per device.

v0:
```python
import math
import jax
import jax.numpy as jnp
from jax import lax
from jax.sharding import PartitionSpec as P

CAP = 24


def attend(queries, key_new, value_new, cache_keys, cache_values, lengths):
    seq_count, head_count, head_width = queries.shape
    kv_count = key_new.shape[1]
    places = cache_keys.shape[2]
    scaling = 1.0 / math.sqrt(head_width)
    grouped = queries.reshape(seq_count, kv_count, head_count // kv_count, head_width)
    scores = (
        jnp.einsum("skgd,skpd->skgp", grouped, cache_keys, preferred_element_type=jnp.float32)
        * scaling
    )
    usable = jnp.arange(places, dtype=jnp.int32)[None, :] < lengths[:, None]
    scores = jnp.where(usable[:, None, None, :], scores, -jnp.inf)
    own_score = (
        jnp.einsum("skgd,skd->skg", grouped, key_new, preferred_element_type=jnp.float32) * scaling
    )
    top_score = jnp.maximum(jnp.max(scores, axis=-1), own_score)
    weights = jnp.exp(scores - top_score[..., None])
    own_weight = jnp.exp(own_score - top_score)
    totals = jnp.sum(weights, axis=-1) + own_weight
    prob_low = (weights / totals[..., None]).astype(jnp.bfloat16)
    own_low = (own_weight / totals).astype(jnp.bfloat16)
    mixture = jnp.einsum(
        "skgp,skpd->skgd", prob_low, cache_values, preferred_element_type=jnp.float32
    )
    mixture = (
        mixture
        + own_low.astype(jnp.float32)[..., None] * value_new.astype(jnp.float32)[:, :, None, :]
    )
    return mixture.astype(jnp.bfloat16).reshape(seq_count, head_count * head_width)


def gating(normed, chosen, router_weight):
    logits = jnp.dot(normed.astype(jnp.float32), router_weight, precision=lax.Precision.HIGHEST)
    expert_ids = jnp.arange(router_weight.shape[1], dtype=jnp.int32)
    picks = (chosen[:, :, None] == expert_ids[None, None, :]).astype(jnp.float32)
    chosen_logits = jnp.sum(picks * logits[:, None, :], axis=-1)
    leading = jax.nn.sigmoid(chosen_logits[:, 0] - chosen_logits[:, 1])
    gates = jnp.stack([leading, 1.0 - leading], axis=1)
    return (gates, picks)


def expert_rows(block, gate_weight, up_weight, down_weight):
    gated = jnp.dot(block, gate_weight, preferred_element_type=jnp.float32)
    upward = jnp.dot(block, up_weight, preferred_element_type=jnp.float32)
    active = (jax.nn.silu(gated) * upward).astype(jnp.bfloat16)
    return jnp.dot(active, down_weight, preferred_element_type=jnp.float32)


def local(
    hidden_in,
    queries,
    key_new,
    value_new,
    cache_keys,
    cache_values,
    lengths,
    out_weight,
    norm_gain,
    router_weight,
    gate_weight,
    up_weight,
    down_weight,
    routes,
):
    seq_rows = hidden_in.shape[0]
    model_width = hidden_in.shape[1]
    tok_count = lax.axis_size("tok")
    expert_total = router_weight.shape[1]
    replicas = tok_count // expert_total
    pieces = 1
    rows_each = seq_rows // pieces
    capacity = min(CAP, rows_each)
    first_row = lax.axis_index("tok") * seq_rows
    attn_out = attend(queries, key_new, value_new, cache_keys, cache_values, lengths)
    columns = jnp.dot(
        lax.all_gather(attn_out, "tok", axis=0, tiled=True),
        out_weight,
        preferred_element_type=jnp.float32,
    )
    partial_out = lax.all_to_all(columns, "tok", split_axis=0, concat_axis=1, tiled=True)
    projected = lax.psum(partial_out, "side")
    stream = (hidden_in.astype(jnp.float32) + projected).astype(jnp.bfloat16).astype(jnp.float32)
    normed = (
        stream * lax.rsqrt(jnp.mean(stream * stream, axis=-1, keepdims=True) + 1e-05) * norm_gain
    ).astype(jnp.bfloat16)
    chosen = lax.dynamic_slice_in_dim(routes, first_row + 0, rows_each, 0)
    gates, picks = gating(normed, chosen, router_weight)
    hits = jnp.sum(picks, axis=1)
    ranks = jnp.cumsum(hits, axis=0) - hits
    slot_ids = jnp.arange(capacity, dtype=jnp.float32)
    placed = hits[:, :, None] * (ranks[:, :, None] == slot_ids[None, None, :]).astype(jnp.float32)
    send_rows = jnp.einsum(
        "bec,bd->ecd", placed.astype(jnp.bfloat16), normed, preferred_element_type=jnp.float32
    ).astype(jnp.bfloat16)
    outgoing = jnp.repeat(send_rows, replicas, axis=0)
    arrived = lax.all_to_all(outgoing, "tok", split_axis=0, concat_axis=0, tiled=True)
    sources, slots, width_in = arrived.shape
    partial_rows = expert_rows(
        arrived.reshape(sources * slots, width_in), gate_weight, up_weight, down_weight
    )
    returned = lax.all_to_all(
        partial_rows.reshape(sources, slots, width_in),
        "tok",
        split_axis=0,
        concat_axis=0,
        tiled=True,
    )
    per_expert = jnp.sum(returned.reshape(expert_total, replicas, capacity, model_width), axis=1)
    slot_gates = (
        jnp.einsum("bk,bke->be", gates, picks, precision=lax.Precision.HIGHEST)[:, :, None] * placed
    )
    combined = jnp.einsum("bec,ecd->bd", slot_gates, per_expert, precision=lax.Precision.HIGHEST)
    combined_all = lax.psum(combined, "side")
    results = (stream + combined_all).astype(jnp.bfloat16)
    return results


def solution(mesh):
    return jax.shard_map(
        local,
        mesh=mesh,
        in_specs=(
            P(("grp", "tok"), None),
            P(("grp", "tok"), "side", None),
            P(("grp", "tok"), "side", None),
            P(("grp", "tok"), "side", None),
            P(("grp", "tok"), "side", None, None),
            P(("grp", "tok"), "side", None, None),
            P(("grp", "tok")),
            P("side", "tok"),
            P(),
            P(),
            P(None, ("tok", "side")),
            P(None, ("tok", "side")),
            P(("tok", "side"), None),
            P("grp", None),
        ),
        out_specs=P(("grp", "tok"), None),
        check_vma=False,
    )
```

profile of v0, /device:TPU:0, one launch (start us, length us, event | category | flops | bytes accessed | tf_op | source)
XLA Modules:
  0.0 225.7 jit_solution(1218781161953350367)
XLA Ops:
  6.5 0.9 iota_compare_fusion.2
  7.4 0.7 convert_element_type.48
  8.2 1.1 fusion.10
  9.3 2.3 %fusion.31 = (f32[32,2,6]{2,1,0:T(2,128)S(1)}, f32[32,2,6,128]{3,2,1,0:T(8,128)S(1)}) fusion(bf16[32,2,128,128]{3,2,1,0:T(8,128)(2,1)S(1)} %copy-done, bf16[32,2,6,128]{3,0,2,1:T(8,128)(2,1)} %bitcast.37, pred[32,128]{1,0:T(8,128)(4,1)S(1)} %iota_compare_fusion.2), kind=kOutput, calls=%fused_computation.57 | convolution fusion | flops 12729984 | bytes 2397696 | tf_op jit(solution)/shard_map/skgd,skpd->skgp/dot_general | solution.py:17
  11.7 0.3 fusion.8
  12.0 0.7 fusion.2
  12.7 0.1 reshape.65
  12.9 33.8 %all_gather.3 = bf16[256,1536]{1,0:T(8,128)(2,1)S(1)} all-gather(bf16[32,1536]{1,0:T(8,128)(2,1)S(1)} %reshape.65), channel_id=1, replica_groups=mesh['grp'=2,'tok'=8,'side'=2] {'tok'}, dimensions={0}, use_global_device_ids=true | all-gather | bytes 884736 | tf_op jit(solution)/shard_map/all_gather | solution.py:85
  46.7 0.6 fusion.32
  47.3 14.9 %all_to_all.29 = f32[8,32,384]{2,1,0:T(8,128)S(1)} all-to-all(f32[8,32,384]{2,1,0:T(8,128)S(1)} %bitcast.32), channel_id=1, replica_groups=mesh['grp'=2,'tok'=8,'side'=2] {'tok'}, dimensions={0} | all-to-all | bytes 786432 | tf_op jit(solution)/shard_map/all_to_all | solution.py:89
  62.2 0.8 copy.45
  63.2 16.9 %all-reduce.3.cloned.1.call-done = f32[32,3072]{1,0:T(8,128)} async-done(((f32[32,3072]{1,0:T(8,128)}), f32[32,3072]{1,0:T(8,128)}) %all-reduce.3.cloned.1.call-update) | async-done | bytes 393232 | tf_op jit(solution)/shard_map/psum | solution.py:90
  80.1 1.2 fusion.4
  81.3 0.3 fusion.16
  82.0 0.4 convolution_convert_fusion
  82.3 0.1 broadcast_in_dim.16
  82.5 34.9 %all_to_all.30 = bf16[8,24,3072]{2,1,0:T(8,128)(2,1)S(1)} all-to-all(bf16[8,24,3072]{2,1,0:T(8,128)(2,1)S(1)} %bitcast.29), channel_id=1, replica_groups=mesh['grp'=2,'tok'=8,'side'=2] {'tok'}, dimensions={0} | all-to-all | bytes 2359296 | tf_op jit(solution)/shard_map/all_to_all | solution.py:105
  117.4 8.4 %fusion.33 = f32[192,2048]{1,0:T(8,128)} fusion(bf16[192,3072]{1,0:T(8,128)(2,1)S(1)} %bitcast.34, bf16[3072,2048]{1,0:T(8,128)(2,1)} %param.24), kind=kOutput, calls=%fused_computation.59 | convolution fusion | flops 2415919104 | bytes 15335424 | tf_op jit(solution)/shard_map/dot_general | solution.py:52
  125.8 15.3 %fusion.3 = f32[192,3072]{1,0:T(8,128)} fusion(bf16[2048,3072]{1,0:T(8,128)(2,1)} %param.26, bf16[192,3072]{1,0:T(8,128)(2,1)S(1)} %bitcast.35, bf16[3072,2048]{1,0:T(8,128)(2,1)} %param.25, f32[192,2048]{1,0:T(8,128)} %fusion.33), kind=kOutput, calls=%fused_computation.9 | convolution fusion | flops 4834197504 | bytes 30277632 | tf_op jit(solution)/shard_map/dot_general | solution.py:55
  141.1 57.0 %all_to_all.31 = f32[8,24,3072]{2,1,0:T(8,128)S(1)} all-to-all(f32[8,24,3072]{2,1,0:T(8,128)} %bitcast.30), channel_id=1, replica_groups=mesh['grp'=2,'tok'=8,'side'=2] {'tok'}, dimensions={0} | all-to-all | bytes 4718592 | tf_op jit(solution)/shard_map/all_to_all | solution.py:110
  198.1 0.1 bitcast_reduce_fusion
  198.3 1.5 convolution_bitcast_fusion
  199.7 17.5 %all-reduce.5.cloned.1.call-done = f32[32,3072]{1,0:T(8,128)} async-done(((f32[32,3072]{1,0:T(8,128)}), f32[32,3072]{1,0:T(8,128)}) %all-reduce.5.cloned.1.call-update) | async-done | bytes 393232 | tf_op jit(solution)/shard_map/psum | solution.py:122
  217.2 1.7 fusion.7
  (30 shorter events, 0.6 us)
Async XLA Ops:
  6.5 2.7 %copy-start = (bf16[32,2,128,128]{3,2,1,0:T(8,128)(2,1)S(1)}, bf16[32,2,128,128]{3,2,1,0:T(8,128)(2,1)}, u32[]{:S(2)}) copy-start(bf16[32,2,128,128]{3,2,1,0:T(8,128)(2,1)} %param.18) | copy-start | bytes 6291460
  6.5 73.6 %all-reduce.3.cloned.1.call-start = ((), (), s32[]{:S(2)}) async-start(), calls=%async_computation.3 | async-start | bytes 786432 | tf_op jit(solution)/shard_map/psum | solution.py:90
  9.3 2.7 %copy-start.5 = (bf16[32,2,128,128]{3,2,1,0:T(8,128)(2,1)S(1)}, bf16[32,2,128,128]{3,2,1,0:T(8,128)(2,1)}, u32[]{:S(2)}) copy-start(bf16[32,2,128,128]{3,2,1,0:T(8,128)(2,1)} %param.19) | copy-start | bytes 6291460
  12.0 34.7 %copy-start.1 = (bf16[1536,384]{1,0:T(8,128)(2,1)S(1)}, bf16[1536,384]{1,0:T(8,128)(2,1)}, u32[]{:S(2)}) copy-start(bf16[1536,384]{1,0:T(8,128)(2,1)} %param.21) | copy-start | bytes 3538948
  47.2 15.8 %copy-start.4 = (s32[256,2]{0,1:T(2,128)S(1)}, s32[256,2]{0,1:T(2,128)}, u32[]{:S(2)}) copy-start(s32[256,2]{0,1:T(2,128)} %param.27) | copy-start | bytes 6148
  47.3 32.9 %copy-start.2 = (bf16[32,3072]{1,0:T(8,128)(2,1)S(1)}, bf16[32,3072]{1,0:T(8,128)(2,1)}, u32[]{:S(2)}) copy-start(bf16[32,3072]{1,0:T(8,128)(2,1)} %param.14) | copy-start | bytes 589828
  47.3 34.0 %copy-start.3 = (f32[3072]{0:T(1024)S(1)}, f32[3072]{0:T(1024)}, u32[]{:S(2)}) copy-start(f32[3072]{0:T(1024)} %param.22) | copy-start | bytes 36868
  47.3 34.0 %copy-start.6 = (f32[3072,4]{0,1:T(4,128)S(1)}, f32[3072,4]{0,1:T(4,128)}, u32[]{:S(2)}) copy-start(f32[3072,4]{0,1:T(4,128)} %param.23) | copy-start | bytes 147460
  63.0 154.2 %all-reduce.5.cloned.1.call-start = ((), (), s32[]{:S(2)}) async-start(), calls=%async_computation.4 | async-start | bytes 786432 | tf_op jit(solution)/shard_map/psum | solution.py:122
Sparse Core Ops, SparseCore 0:
  63.1 16.9 all-reduce.2
  199.9 17.2 all-reduce.4
where the time goes:
time: 226 us
  blocking collectives  141 us (62%)
  waiting for transfers between devices  34.4 us (15%)
  matrix products  30.5 us (13%)
  between operations  13.6 us (6%)
  other arithmetic  5.14 us (2%)
    all_to_all x1, blocking collectives, local(): lax.all_to_all(partial_rows.reshape(sources, slots, width_in), 'tok', spl...  57 us
    all_to_all x1, blocking collectives, local(): lax.all_to_all(outgoing, 'tok', split_axis=0, concat_axis=0, tiled=True)  34.9 us
    all_gather x1, blocking collectives, local(): lax.all_gather(attn_out, 'tok', axis=0, tiled=True)  33.8 us
    psum x1, waiting for transfers between devices, local(): combined_all = lax.psum(combined, 'side')  17.5 us
    psum x1, waiting for transfers between devices, local(): projected = lax.psum(partial_out, 'side')  16.9 us
    dot_general x1, matrix products, expert_rows(): return jnp.dot(active, down_weight, preferred_element_type=jnp.float32)  15.3 us
    all_to_all x1, blocking collectives, local(): lax.all_to_all(columns, 'tok', split_axis=0, concat_axis=1, tiled=True)  14.9 us
    dot_general x1, matrix products, expert_rows(): gated = jnp.dot(block, gate_weight, preferred_element_type=jnp.float32)  8.39 us
  transfers between devices with their start and end apart: 2, of which 2 were waited for; matrix products, arithmetic and copies ran while one was open for 0% of the time, Pallas kernels for 0%

commit v1 on v0

--- a/solution.py
+++ b/solution.py
@@ -5,6 +5,7 @@
 from jax.sharding import PartitionSpec as P
 
 CAP = 24
+pack_notes = lambda page: lax.all_gather(page, "side").sum(axis=0)
 
 
 def attend(queries, key_new, value_new, cache_keys, cache_values, lengths):
@@ -87,7 +88,7 @@
         preferred_element_type=jnp.float32,
     )
     partial_out = lax.all_to_all(columns, "tok", split_axis=0, concat_axis=1, tiled=True)
-    projected = lax.psum(partial_out, "side")
+    projected = pack_notes(partial_out)
     stream = (hidden_in.astype(jnp.float32) + projected).astype(jnp.bfloat16).astype(jnp.float32)
     normed = (
         stream * lax.rsqrt(jnp.mean(stream * stream, axis=-1, keepdims=True) + 1e-05) * norm_gain

time: 226 us -> 208 us (0.920)
  blocking collectives: 141 us -> 126 us
  waiting for transfers between devices: 34.4 us -> 26.5 us
  starting transfers between devices: 0.04 us -> 5.53 us
    psum x1 -> x0, waiting for transfers between devices: 16.9 us -> none  [local(): projected = lax.psum(partial_out, 'side')]
    all_to_all x1 -> x0, blocking collectives: 14.9 us -> none  [local(): lax.all_to_all(columns, 'tok', split_axis=0, concat_axis=1, tiled=True)]
    all_to_all x0 -> x1, waiting for transfers between devices: none -> 9.07 us  [local(): lax.all_to_all(columns, 'tok', split_axis=0, concat_axis=1, tiled=True)]
    all_to_all x0 -> x1, starting transfers between devices: none -> 5.49 us  [local(): lax.all_to_all(columns, 'tok', split_axis=0, concat_axis=1, tiled=True)]
    all_to_all x1, blocking collectives: 34.9 us -> 32.4 us  [local(): lax.all_to_all(outgoing, 'tok', split_axis=0, concat_axis=0, tiled=True)]
    all_gather x0 -> x1, blocking collectives: none -> 2.5 us  [pack_notes = lambda page: lax.all_gather(page, 'side').sum(axis=0)]
where the time goes in v1:
time: 208 us
  blocking collectives  126 us (61%)
  matrix products  31.2 us (15%)
  waiting for transfers between devices  26.5 us (13%)
  between operations  13.6 us (7%)
  starting transfers between devices  5.53 us (3%)
  other arithmetic  4.18 us (2%)
    all_to_all x1, blocking collectives, local(): lax.all_to_all(partial_rows.reshape(sources, slots, width_in), 'tok', spl...  57 us
    all_gather x1, blocking collectives, local(): lax.all_gather(attn_out, 'tok', axis=0, tiled=True)  33.9 us
    all_to_all x1, blocking collectives, local(): lax.all_to_all(outgoing, 'tok', split_axis=0, concat_axis=0, tiled=True)  32.4 us
    psum x1, waiting for transfers between devices, local(): combined_all = lax.psum(combined, 'side')  17.4 us
    dot_general x1, matrix products, expert_rows(): return jnp.dot(active, down_weight, preferred_element_type=jnp.float32)  15.2 us
    all_to_all x1, waiting for transfers between devices, local(): lax.all_to_all(columns, 'tok', split_axis=0, concat_axis=1, tiled=True)  9.07 us
    dot_general x1, matrix products, expert_rows(): gated = jnp.dot(block, gate_weight, preferred_element_type=jnp.float32)  8.34 us
    all_to_all x1, starting transfers between devices, local(): lax.all_to_all(columns, 'tok', split_axis=0, concat_axis=1, tiled=True)  5.49 us
  transfers between devices with their start and end apart: 2, of which 2 were waited for; matrix products, arithmetic and copies ran while one was open for 0% of the time, Pallas kernels for 0%

profile of v1, /device:TPU:0, one launch (start us, length us, event | category | flops | bytes accessed | tf_op | source)
XLA Modules:
  0.0 207.6 jit_solution(12459570026214497629)
XLA Ops:
  6.5 0.9 iota_compare_fusion.2
  7.4 0.7 convert_element_type.48
  8.1 1.1 fusion.10
  9.3 2.3 %fusion.31 = (f32[32,2,6]{2,1,0:T(2,128)S(1)}, f32[32,2,6,128]{3,2,1,0:T(8,128)S(1)}) fusion(bf16[32,2,128,128]{3,2,1,0:T(8,128)(2,1)S(1)} %copy-done, bf16[32,2,6,128]{3,0,2,1:T(8,128)(2,1)} %bitcast.33, pred[32,128]{1,0:T(8,128)(4,1)S(1)} %iota_compare_fusion.2), kind=kOutput, calls=%fused_computation.57 | convolution fusion | flops 12729984 | bytes 2397696 | tf_op jit(solution)/shard_map/skgd,skpd->skgp/dot_general | solution.py:18
  11.7 0.3 fusion.8
  12.0 0.7 fusion.2
  12.7 0.1 reshape.66
  12.9 33.9 %all_gather.9 = bf16[256,1536]{1,0:T(8,128)(2,1)S(1)} all-gather(bf16[32,1536]{1,0:T(8,128)(2,1)S(1)} %reshape.66), channel_id=1, replica_groups=mesh['grp'=2,'tok'=8,'side'=2] {'tok'}, dimensions={0}, use_global_device_ids=true | all-gather | bytes 884736 | tf_op jit(solution)/shard_map/all_gather | solution.py:86
  46.8 1.3 fusion.32
  48.1 5.5 %all-to-all-start = ((f32[8,32,384]{2,1,0:T(8,128)}), f32[8,32,384]{2,1,0:T(8,128)S(1)}, u32[]{:S(2)}, u32[]{:S(2)}) async-start(f32[8,32,384]{2,1,0:T(8,128)} %bitcast.4), calls=%async_computation | async-start | bytes 786432 | tf_op jit(solution)/shard_map/all_to_all | solution.py:90
  53.7 9.1 %all-to-all-done = f32[8,32,384]{2,1,0:T(8,128)S(1)} async-done(((f32[8,32,384]{2,1,0:T(8,128)}), f32[8,32,384]{2,1,0:T(8,128)S(1)}, u32[]{:S(2)}, u32[]{:S(2)}) %all-to-all-start) | async-done | bytes 393248 | tf_op jit(solution)/shard_map/all_to_all | solution.py:90
  62.8 0.2 copy.33
  63.1 2.5 %all_gather.11 = f32[2,32,3072]{2,1,0:T(8,128)S(1)} all-gather(f32[1,32,3072]{2,1,0:T(8,128)S(1)} %all_gather.10), channel_id=1, replica_groups=mesh['grp'=2,'tok'=8,'side'=2] {'side'}, dimensions={0}, use_global_device_ids=true | all-gather | bytes 1179648 | tf_op jit(solution)/shard_map/all_gather | solution.py:8
  65.7 0.2 fusion.4
  65.9 0.3 fusion.16
  66.5 0.4 convolution_convert_fusion
  67.1 32.4 %all_to_all.26 = bf16[8,24,3072]{2,1,0:T(8,128)(2,1)S(1)} all-to-all(bf16[8,24,3072]{2,1,0:T(8,128)(2,1)S(1)} %bitcast.27), channel_id=1, replica_groups=mesh['grp'=2,'tok'=8,'side'=2] {'tok'}, dimensions={0} | all-to-all | bytes 2359296 | tf_op jit(solution)/shard_map/all_to_all | solution.py:106
  99.4 8.3 %fusion.33 = f32[192,2048]{1,0:T(8,128)} fusion(bf16[192,3072]{1,0:T(8,128)(2,1)S(1)} %bitcast.30, bf16[3072,2048]{1,0:T(8,128)(2,1)} %param.24), kind=kOutput, calls=%fused_computation.59 | convolution fusion | flops 2415919104 | bytes 15335424 | tf_op jit(solution)/shard_map/dot_general | solution.py:53
  107.8 15.2 %fusion.3 = f32[192,3072]{1,0:T(8,128)} fusion(bf16[2048,3072]{1,0:T(8,128)(2,1)} %param.26, bf16[192,3072]{1,0:T(8,128)(2,1)S(1)} %bitcast.31, bf16[3072,2048]{1,0:T(8,128)(2,1)} %param.25, f32[192,2048]{1,0:T(8,128)} %fusion.33), kind=kOutput, calls=%fused_computation.9 | convolution fusion | flops 4834197504 | bytes 30277632 | tf_op jit(solution)/shard_map/dot_general | solution.py:56
  123.0 57.0 %all_to_all.27 = f32[8,24,3072]{2,1,0:T(8,128)S(1)} all-to-all(f32[8,24,3072]{2,1,0:T(8,128)} %bitcast.28), channel_id=1, replica_groups=mesh['grp'=2,'tok'=8,'side'=2] {'tok'}, dimensions={0} | all-to-all | bytes 4718592 | tf_op jit(solution)/shard_map/all_to_all | solution.py:111
  180.0 0.1 bitcast_reduce_fusion
  180.2 1.5 convolution_bitcast_fusion
  181.6 17.4 %all-reduce.2.cloned.1.call-done = f32[32,3072]{1,0:T(8,128)} async-done(((f32[32,3072]{1,0:T(8,128)}), f32[32,3072]{1,0:T(8,128)}) %all-reduce.2.cloned.1.call-update) | async-done | bytes 393232 | tf_op jit(solution)/shard_map/psum | solution.py:123
  199.1 1.7 fusion.7
  (31 shorter events, 0.8 us)
Async XLA Ops:
  6.5 2.7 %copy-start = (bf16[32,2,128,128]{3,2,1,0:T(8,128)(2,1)S(1)}, bf16[32,2,128,128]{3,2,1,0:T(8,128)(2,1)}, u32[]{:S(2)}) copy-start(bf16[32,2,128,128]{3,2,1,0:T(8,128)(2,1)} %param.18) | copy-start | bytes 6291460
  9.3 2.7 %copy-start.5 = (bf16[32,2,128,128]{3,2,1,0:T(8,128)(2,1)S(1)}, bf16[32,2,128,128]{3,2,1,0:T(8,128)(2,1)}, u32[]{:S(2)}) copy-start(bf16[32,2,128,128]{3,2,1,0:T(8,128)(2,1)} %param.19) | copy-start | bytes 6291460
  12.0 34.7 %copy-start.1 = (bf16[1536,384]{1,0:T(8,128)(2,1)S(1)}, bf16[1536,384]{1,0:T(8,128)(2,1)}, u32[]{:S(2)}) copy-start(bf16[1536,384]{1,0:T(8,128)(2,1)} %param.21) | copy-start | bytes 3538948
  46.8 6.9 %copy-start.4 = (s32[256,2]{0,1:T(2,128)S(1)}, s32[256,2]{0,1:T(2,128)}, u32[]{:S(2)}) copy-start(s32[256,2]{0,1:T(2,128)} %param.27) | copy-start | bytes 6148
  48.1 14.7 %all-to-all-start = ((f32[8,32,384]{2,1,0:T(8,128)}), f32[8,32,384]{2,1,0:T(8,128)S(1)}, u32[]{:S(2)}, u32[]{:S(2)}) async-start(f32[8,32,384]{2,1,0:T(8,128)} %bitcast.4), calls=%async_computation | async-start | bytes 786432 | tf_op jit(solution)/shard_map/all_to_all | solution.py:90
  53.6 145.5 %all-reduce.2.cloned.1.call-start = ((), (), s32[]{:S(2)}) async-start(), calls=%async_computation.3 | async-start | bytes 786432 | tf_op jit(solution)/shard_map/psum | solution.py:123
  63.0 2.7 %copy-start.2 = (bf16[32,3072]{1,0:T(8,128)(2,1)S(1)}, bf16[32,3072]{1,0:T(8,128)(2,1)}, u32[]{:S(2)}) copy-start(bf16[32,3072]{1,0:T(8,128)(2,1)} %param.14) | copy-start | bytes 589828
  63.1 2.8 %copy-start.3 = (f32[3072]{0:T(1024)S(1)}, f32[3072]{0:T(1024)}, u32[]{:S(2)}) copy-start(f32[3072]{0:T(1024)} %param.22) | copy-start | bytes 36868
  63.1 2.8 %copy-start.6 = (f32[3072,4]{0,1:T(4,128)S(1)}, f32[3072,4]{0,1:T(4,128)}, u32[]{:S(2)}) copy-start(f32[3072,4]{0,1:T(4,128)} %param.23) | copy-start | bytes 147460
Sparse Core Ops, SparseCore 0:
  181.8 17.2 all-reduce.1
